TPU v7x, 32 devices: a whole 2x2x4 slice. The times are simulated.
32 devices in a mesh: row: 4 (over z), col: 8 (over y, x, core).
Axes of the slice: x: 2, y: 2, z: 4, core: 2. Of those that a mesh axis runs over, the one named last changes fastest.
Arguments:
- tri_panels: float32 [8192, 4096], P('row', 'col'), may hold values from -1 to 2, as said below
- rhs_rows: float32 [8192, 1024], P(('row', 'col')), may hold values from -6 to 6
Outputs:
- rhs_grid: float32 [8192, 1024], P('row', 'col')
Inputs may be any that keep to these rules, and one draw needn't show every extreme that they name: `tri_panels`: in L's row order the entries above the diagonal are zero and the diagonal entries are positive.
All inputs are finite; a program needn't handle non-finite values.
Results may differ from a plain program's by a relative error of at most 0.00011.
Values sent between devices are 32-bit elements; how exact they have to be, the bound alone decides.
A program may use at most 256 MiB of HBM per device.

v0:
```python
import jax
import jax.numpy as jnp
from jax import lax
from jax.sharding import PartitionSpec as P


def broadcast(block, axis, source):
    block = jnp.where(lax.axis_index(axis) == source, block, jnp.zeros_like(block))
    return lax.psum(block, axis)


def on_device(tri_panels, rhs_rows):
    row_count = lax.axis_size("row")
    col_count = lax.axis_size("col")
    row_position = lax.axis_index("row")
    col_position = lax.axis_index("col")
    local_rows, block_size = tri_panels.shape
    blocks = local_rows // block_size
    sub_rows = block_size // col_count
    parted = rhs_rows.reshape(blocks, sub_rows, rhs_rows.shape[1])
    state_rhs = lax.all_to_all(parted, "col", split_axis=2, concat_axis=1, tiled=True)
    identity_block = jnp.eye(block_size, dtype=jnp.float32)
    own_pieces = tri_panels.reshape(blocks, block_size, block_size)
    own_diag = lax.dynamic_index_in_dim(own_pieces, col_position // row_count, 0, keepdims=False)
    own_diag = jnp.where(col_position % row_count == row_position, own_diag, identity_block)
    own_inverse = jax.scipy.linalg.solve_triangular(own_diag, identity_block, lower=True)

    def advance(state_rhs, panel_cols, inverse_block, step_index, first_slot):
        count = blocks - first_slot
        owner_row = step_index % row_count
        slot_index = step_index // row_count
        pieces = panel_cols.reshape(count, block_size, block_size)
        current = lax.dynamic_index_in_dim(state_rhs, slot_index, 0, keepdims=False)
        local_solution = jnp.dot(
            inverse_block,
            current,
            precision=lax.Precision.HIGHEST,
            preferred_element_type=jnp.float32,
        )
        solution = broadcast(local_solution, "row", owner_row)
        stored = jnp.where(row_position == owner_row, solution, current)
        state_rhs = lax.dynamic_update_index_in_dim(state_rhs, stored, slot_index, 0)
        global_block = (first_slot + jnp.arange(count, dtype=jnp.int32)) * row_count + row_position
        product = jnp.einsum("sij,jc->sic", pieces, solution, precision=lax.Precision.HIGHEST)
        trailing = state_rhs[first_slot:]
        trailing = jnp.where(
            (global_block > step_index)[:, None, None], trailing - product, trailing
        )
        if first_slot > 0:
            return jnp.concatenate([state_rhs[:first_slot], trailing], 0)
        return trailing

    group_count = (col_count + row_count - 1) // row_count
    everything, inverses = (
        lax.all_gather(tri_panels, "col", axis=1, tiled=True),
        lax.all_gather(own_inverse, "col", axis=1, tiled=True),
    )
    for first_slot in range(group_count):
        begin_step = first_slot * row_count
        end_step = min(begin_step + row_count, col_count)
        own_rows = everything[first_slot * block_size :]

        def upfront_step(step_index, state_rhs, own_rows=own_rows, first_slot=first_slot):
            panel_cols = lax.dynamic_slice_in_dim(own_rows, step_index * block_size, block_size, 1)
            inverse_block = lax.dynamic_slice_in_dim(
                inverses, step_index * block_size, block_size, 1
            )
            return advance(state_rhs, panel_cols, inverse_block, step_index, first_slot)

        state_rhs = lax.fori_loop(begin_step, end_step, upfront_step, state_rhs)
    return state_rhs.reshape(local_rows, state_rhs.shape[2])


def solution(mesh):
    return jax.shard_map(
        on_device,
        mesh=mesh,
        in_specs=(P("row", "col"), P(("row", "col"), None)),
        out_specs=P("row", "col"),
        check_vma=False,
    )
```

profile of v0, /device:TPU:16, one launch (start us, length us, event | category | flops | bytes accessed | tf_op | source)
XLA Modules:
  0.0 597.4 jit_solution(16486143902981897702)
XLA Ops:
  8.7 8.0 %while.33 = (s32[]{:T(128)}, f32[512,512]{1,0:T(8,128)S(1)}, s32[4,2]{0,1:T(2,128)S(1)}, f32[4,128,128]{2,1,0:T(8,128)S(1)}, s32[]{:T(128)}) while((s32[]{:T(128)}, f32[512,512]{1,0:T(8,128)S(1)}, s32[4,2]{0,1:T(2,128)S(1)}, f32[4,128,128]{2,1,0:T(8,128)S(1)}, s32[]{:T(128)}) %tuple.81), condition=%wide.while_cond, body=%wide.while_body.sunk | while | flops 2 | bytes 131181 | solution.py:26
  16.7 39.3 %custom-call.4 = f32[4,128,128]{1,2,0:T(8,128)S(1)} custom-call(f32[4,128,128]{2,1,0:T(8,128)S(1)} %get-tuple-element.284), custom_call_target="InvertDiagBlocksLowerTriangular" | custom-call | tf_op jit(solution)/shard_map/jit(_solve_triangular)/triangular_solve | solution.py:26
  67.8 20.6 %all-to-all-done = f32[8,1,32768]{2,1,0:T(1,128)S(1)} async-done(((f32[8,1,32768]{2,1,0:T(1,128)}), f32[8,1,32768]{2,1,0:T(1,128)S(1)}, u32[]{:S(2)}, u32[]{:S(2)}) %all-to-all-start) | async-done | bytes 1048608 | tf_op jit(solution)/shard_map/all_to_all | solution.py:21
  94.3 81.4 %all-gather.5.cloned.1.call-done = f32[2048,4096]{1,0:T(8,128)} async-done(((f32[2048,512]{1,0:T(8,128)}), f32[2048,4096]{1,0:T(8,128)}) %all-gather.5.cloned.1.call-update) | async-done | bytes 33554448 | tf_op jit(solution)/shard_map/all_gather | solution.py:55
  175.8 17.4 %slice.70 = f32[1536,4096]{1,0:T(8,128)} slice(f32[2048,4096]{1,0:T(8,128)} %all-gather.5.cloned.1.call-done), slice={[512:2048], [0:4096]} | slice | bytes 50331648 | tf_op jit(solution)/shard_map/slice | solution.py:61
  193.2 38.8 %all-gather.3.cloned.1.call-done = f32[512,4096]{1,0:T(8,128)} async-done(((f32[512,512]{1,0:T(8,128)}), f32[512,4096]{1,0:T(8,128)}) %all-gather.3.cloned.1.call-update) | async-done | bytes 8388624 | tf_op jit(solution)/shard_map/all_gather | solution.py:56
  232.1 176.6 %while.31 = (s32[]{:T(128)}, f32[4,512,128]{2,1,0:T(8,128)S(1)}, s32[]{:T(128)}, f32[512,4096]{1,0:T(8,128)}, f32[2048,4096]{1,0:T(8,128)}, /*index=5*/s32[]{:T(...) while((s32[]{:T(128)}, f32[4,512,128]{2,1,0:T(8,128)S(1)}, ...), condition=%wide.region_2.3_spmd, body=%wide.region_0.2_spmd.sunk | while | flops 2013986816 | bytes 19399112 | solution.py:70
  235.1 4.6 constant_dynamic-slice_fusion.11
  239.7 30.8 %all-reduce.3.cloned.1.call-done = f32[512,128]{1,0:T(8,128)} async-done(((f32[512,128]{1,0:T(8,128)}), f32[512,128]{1,0:T(8,128)}) %all-reduce.3.cloned.1.call-update) | async-done | bytes 262160 | tf_op jit(solution)/shard_map/while/body/eval_jaxpr/psum | solution.py:9
  270.5 5.2 subtract_select_fusion.2
  278.9 4.6 constant_dynamic-slice_fusion.11
  283.5 30.9 %all-reduce.3.cloned.1.call-done = f32[512,128]{1,0:T(8,128)} async-done(((f32[512,128]{1,0:T(8,128)}), f32[512,128]{1,0:T(8,128)}) %all-reduce.3.cloned.1.call-update) | async-done | bytes 262160 | tf_op jit(solution)/shard_map/while/body/eval_jaxpr/psum | solution.py:9
  314.5 5.2 subtract_select_fusion.2
  322.8 4.6 constant_dynamic-slice_fusion.11
  327.5 31.2 %all-reduce.3.cloned.1.call-done = f32[512,128]{1,0:T(8,128)} async-done(((f32[512,128]{1,0:T(8,128)}), f32[512,128]{1,0:T(8,128)}) %all-reduce.3.cloned.1.call-update) | async-done | bytes 262160 | tf_op jit(solution)/shard_map/while/body/eval_jaxpr/psum | solution.py:9
  359.6 5.2 subtract_select_fusion.2
  368.0 4.6 constant_dynamic-slice_fusion.11
  372.6 30.8 %all-reduce.3.cloned.1.call-done = f32[512,128]{1,0:T(8,128)} async-done(((f32[512,128]{1,0:T(8,128)}), f32[512,128]{1,0:T(8,128)}) %all-reduce.3.cloned.1.call-update) | async-done | bytes 262160 | tf_op jit(solution)/shard_map/while/body/eval_jaxpr/psum | solution.py:9
  403.4 5.2 subtract_select_fusion.2
  408.6 180.9 %while.32 = (s32[]{:T(128)}, f32[4,512,128]{2,1,0:T(8,128)S(1)}, s32[]{:T(128)}, f32[512,4096]{1,0:T(8,128)}, f32[1536,4096]{1,0:T(8,128)}, /*index=5*/s32[]{:T(...) while((s32[]{:T(128)}, f32[4,512,128]{2,1,0:T(8,128)S(1)}, ...), condition=%wide.region_5.6_spmd, body=%wide.region_3.5_spmd.sunk | while | flops 1611464704 | bytes 22544948 | solution.py:70
  414.5 34.3 %all-reduce.5.cloned.1.call-done = f32[512,128]{1,0:T(8,128)} async-done(((f32[512,128]{1,0:T(8,128)}), f32[512,128]{1,0:T(8,128)}) %all-reduce.5.cloned.1.call-update) | async-done | bytes 262160 | tf_op jit(solution)/shard_map/while/body/eval_jaxpr/psum | solution.py:9
  460.1 33.4 %all-reduce.5.cloned.1.call-done = f32[512,128]{1,0:T(8,128)} async-done(((f32[512,128]{1,0:T(8,128)}), f32[512,128]{1,0:T(8,128)}) %all-reduce.5.cloned.1.call-update) | async-done | bytes 262160 | tf_op jit(solution)/shard_map/while/body/eval_jaxpr/psum | solution.py:9
  504.8 33.6 %all-reduce.5.cloned.1.call-done = f32[512,128]{1,0:T(8,128)} async-done(((f32[512,128]{1,0:T(8,128)}), f32[512,128]{1,0:T(8,128)}) %all-reduce.5.cloned.1.call-update) | async-done | bytes 262160 | tf_op jit(solution)/shard_map/while/body/eval_jaxpr/psum | solution.py:9
  550.7 33.2 %all-reduce.5.cloned.1.call-done = f32[512,128]{1,0:T(8,128)} async-done(((f32[512,128]{1,0:T(8,128)}), f32[512,128]{1,0:T(8,128)}) %all-reduce.5.cloned.1.call-update) | async-done | bytes 262160 | tf_op jit(solution)/shard_map/while/body/eval_jaxpr/psum | solution.py:9
  (113 shorter events, 87.3 us)
Async XLA Ops:
  6.5 169.3 %all-gather.5.cloned.1.call-start = ((), (), s32[]{:S(2)}) async-start(), calls=%async_computation.2 | async-start | bytes 37748736 | tf_op jit(solution)/shard_map/all_gather | solution.py:55
  7.3 224.8 %all-gather.3.cloned.1.call-start = ((), (), s32[]{:S(2)}) async-start(), calls=%async_computation.1 | async-start | bytes 9437184 | tf_op jit(solution)/shard_map/all_gather | solution.py:56
  56.6 3.8 copy-start.2
  64.1 24.4 %all-to-all-start = ((f32[8,1,32768]{2,1,0:T(1,128)}), f32[8,1,32768]{2,1,0:T(1,128)S(1)}, u32[]{:S(2)}, u32[]{:S(2)}) async-start(f32[8,1,32768]{2,1,0:T(1,128)} %reshape.78), calls=%async_computation | async-start | bytes 2097152 | tf_op jit(solution)/shard_map/all_to_all | solution.py:21
  232.1 38.4 %all-reduce.3.cloned.1.call-start = ((), (), s32[]{:S(2)}) async-start(), calls=%async_computation.3 | async-start | bytes 524288 | tf_op jit(solution)/shard_map/while/body/eval_jaxpr/psum | solution.py:9
  275.8 38.6 %all-reduce.3.cloned.1.call-start = ((), (), s32[]{:S(2)}) async-start(), calls=%async_computation.3 | async-start | bytes 524288 | tf_op jit(solution)/shard_map/while/body/eval_jaxpr/psum | solution.py:9
  319.7 38.9 %all-reduce.3.cloned.1.call-start = ((), (), s32[]{:S(2)}) async-start(), calls=%async_computation.3 | async-start | bytes 524288 | tf_op jit(solution)/shard_map/while/body/eval_jaxpr/psum | solution.py:9
  364.9 38.5 %all-reduce.3.cloned.1.call-start = ((), (), s32[]{:S(2)}) async-start(), calls=%async_computation.3 | async-start | bytes 524288 | tf_op jit(solution)/shard_map/while/body/eval_jaxpr/psum | solution.py:9
  408.9 3.4 copy-start
  408.9 39.9 %all-reduce.5.cloned.1.call-start = ((), (), s32[]{:S(2)}) async-start(), calls=%async_computation.4 | async-start | bytes 524288 | tf_op jit(solution)/shard_map/while/body/eval_jaxpr/psum | solution.py:9
  454.5 3.4 copy-start
  454.5 39.0 %all-reduce.5.cloned.1.call-start = ((), (), s32[]{:S(2)}) async-start(), calls=%async_computation.4 | async-start | bytes 524288 | tf_op jit(solution)/shard_map/while/body/eval_jaxpr/psum | solution.py:9
  499.2 3.4 copy-start
  499.2 39.2 %all-reduce.5.cloned.1.call-start = ((), (), s32[]{:S(2)}) async-start(), calls=%async_computation.4 | async-start | bytes 524288 | tf_op jit(solution)/shard_map/while/body/eval_jaxpr/psum | solution.py:9
  545.1 3.4 copy-start
  545.1 38.8 %all-reduce.5.cloned.1.call-start = ((), (), s32[]{:S(2)}) async-start(), calls=%async_computation.4 | async-start | bytes 524288 | tf_op jit(solution)/shard_map/while/body/eval_jaxpr/psum | solution.py:9
  589.6 1.0 copy-start.1
Sparse Core Ops, SparseCore 0:
  9.2 166.5 all-gather.4
  177.7 54.3 all-gather.2
  235.2 35.2 all-reduce.2
  278.9 35.4 all-reduce.2
  322.9 35.6 all-reduce.2
  368.0 35.2 all-reduce.2
  412.3 36.4 all-reduce.4
  458.0 35.4 all-reduce.4
  502.7 35.6 all-reduce.4
  548.5 35.2 all-reduce.4
where the time goes:
time: 601 us; the launch traced here: 597 us
  waiting for transfers between devices  400 us (67%)
  local copies, waits for them, and re-layouts  64.1 us (11%)
  matrix products  64.1 us (11%)
  other arithmetic  50.3 us (8%)
  between operations  13.6 us (2%)
    psum x8, waiting for transfers between devices, broadcast(): return lax.psum(block, axis)  258 us
    all_gather x1, waiting for transfers between devices, on_device(): lax.all_gather(tri_panels, 'col', axis=1, tiled=True)  81.4 us
    another operation x4, other arithmetic, on_device(): jax.scipy.linalg.solve_triangular(own_diag, identity_block, lower=True)  41.7 us
    all_gather x1, waiting for transfers between devices, on_device(): lax.all_gather(own_inverse, 'col', axis=1, tiled=True)  38.8 us
    dot_general x8, matrix products, advance(): jnp.einsum('sij,jc->sic', pieces, solution, precision=lax.Precision.HIGHEST)  36.6 us
    dynamic_slice x8, local copies, waits for them, and re-layouts, upfront_step(): lax.dynamic_slice_in_dim(own_rows, step_index * block_size, block_size, 1)  27.3 us
    dot_general x8, matrix products, advance(): jnp.dot(inverse_block, current, precision=lax.Precision.HIGHEST, preferre...  24.5 us
    all_to_all x1, waiting for transfers between devices, on_device(): lax.all_to_all(parted, 'col', split_axis=2, concat_axis=1, tiled=True)  20.6 us
  transfers between devices with their start and end apart: 11, of which 11 were waited for; matrix products, arithmetic and copies ran while one was open for 18% of the time, Pallas kernels for 0%

commit v1 on v0

v1 whole, which is shorter than its diff:
```python
import functools

import jax
import jax.numpy as jnp
from jax import lax
from jax.experimental import pallas as pl
from jax.experimental.pallas import tpu as pltpu
from jax.sharding import PartitionSpec as P

HIGHEST = lax.Precision.HIGHEST


def dot(a, b):
    return jnp.dot(a, b, precision=HIGHEST, preferred_element_type=jnp.float32)


def steps_kernel(
    row_count, col_count, panels_ref, inverses_ref, state_in_ref, solved_ref, state_ref,
    panels, inverses, panel_sem, inverse_sem, state_sem, send_sem, recv_sem,
):
    row = lax.axis_index("row")
    slots, size, _ = state_ref.shape

    def panel_copy(k):
        return pltpu.make_async_copy(
            panels_ref.at[:, pl.ds(pl.multiple_of(k * size, size), size)],
            panels.at[k],
            panel_sem.at[k],
        )

    def inverse_copy(s):
        block = jnp.minimum(s * row_count + row, col_count - 1)
        return pltpu.make_async_copy(
            inverses_ref.at[:, pl.ds(pl.multiple_of(block * size, size), size)],
            inverses.at[s],
            inverse_sem.at[s],
        )

    state_copy = pltpu.make_async_copy(state_in_ref, state_ref, state_sem)
    state_copy.start()
    for s in range(slots):
        inverse_copy(s).start()
    for k in range(col_count):
        panel_copy(k).start()

    barrier = pltpu.get_barrier_semaphore()
    for shift in range(1, row_count):
        pl.semaphore_signal(
            barrier, inc=1, device_id={"row": lax.rem(row + shift, row_count)},
            device_id_type=pl.DeviceIdType.MESH,
        )
    pl.semaphore_wait(barrier, row_count - 1)
    state_copy.wait()
    for s in range(slots):
        inverse_copy(s).wait()

    def remote(k, shift):
        return pltpu.make_async_remote_copy(
            src_ref=solved_ref.at[k],
            dst_ref=solved_ref.at[k],
            send_sem=send_sem.at[shift - 1],
            recv_sem=recv_sem.at[k],
            device_id={"row": lax.rem(row + shift, row_count)},
            device_id_type=pl.DeviceIdType.MESH,
        )

    def update(k, s):
        part = panels[k, pl.ds(pl.multiple_of(s * size, size), size), :]
        state_ref[s] = state_ref[s] - dot(part, solved_ref[k])

    def update_all(k, skipped):
        def one(s, carry):
            @pl.when((s * row_count + row > k) & (s != skipped))
            def _():
                update(k, s)

            return carry

        lax.fori_loop(0, slots, one, 0)

    def step(k, carry):
        owner = lax.rem(k, row_count)
        slot = lax.div(k, row_count)

        @pl.when(row == owner)
        def _():
            @pl.when(k > 0)
            def _():
                update(k - 1, slot)

            solved = dot(inverses[slot], state_ref[slot])
            solved_ref[k] = solved
            for shift in range(1, row_count):
                remote(k, shift).start()
            state_ref[slot] = solved

            @pl.when(k > 0)
            def _():
                update_all(k - 1, slot)

        @pl.when(row != owner)
        def _():
            remote(k, 1).wait_recv()

        panel_copy(k).wait()

        @pl.when((row != lax.rem(k + 1, row_count)) | (k == col_count - 1))
        def _():
            update_all(k, -1)

        @pl.when(row == owner)
        def _():
            for shift in range(1, row_count):
                remote(k, shift).wait_send()

        return carry

    lax.fori_loop(0, col_count, step, 0)


def run_steps(panels, inverses, state):
    row_count = lax.axis_size("row")
    slots, size, width = state.shape
    col_count = panels.shape[1] // size
    anywhere = pl.BlockSpec(memory_space=pl.ANY)
    inside = pl.BlockSpec(memory_space=pltpu.VMEM)
    return pl.pallas_call(
        functools.partial(steps_kernel, row_count, col_count),
        out_shape=(
            jax.ShapeDtypeStruct((col_count, size, width), jnp.float32),
            jax.ShapeDtypeStruct((slots, size, width), jnp.float32),
        ),
        in_specs=[anywhere, anywhere, anywhere],
        out_specs=(inside, inside),
        scratch_shapes=[
            pltpu.VMEM((col_count, slots * size, size), jnp.float32),
            pltpu.VMEM((slots, size, size), jnp.float32),
            pltpu.SemaphoreType.DMA((col_count,)),
            pltpu.SemaphoreType.DMA((slots,)),
            pltpu.SemaphoreType.DMA,
            pltpu.SemaphoreType.DMA((row_count - 1,)),
            pltpu.SemaphoreType.DMA((col_count,)),
        ],
        compiler_params=pltpu.CompilerParams(
            collective_id=0, has_side_effects=True, vmem_limit_bytes=48 * 1024 * 1024
        ),
        cost_estimate=pl.CostEstimate(
            flops=60 * size * size * width * 2 * 6, bytes_accessed=24 << 20, transcendentals=0
        ),
    )(panels, inverses, state)


def on_device(tri_panels, rhs_rows):
    row_count = lax.axis_size("row")
    col_count = lax.axis_size("col")
    row_position = lax.axis_index("row")
    col_position = lax.axis_index("col")
    local_rows, size = tri_panels.shape
    blocks = local_rows // size
    sub_rows = size // col_count
    slots = min((col_count + row_count - 1) // row_count, blocks)
    parted = rhs_rows.reshape(blocks, sub_rows, rhs_rows.shape[1])
    state_rhs = lax.all_to_all(parted, "col", split_axis=2, concat_axis=1, tiled=True)
    identity_block = jnp.eye(size, dtype=jnp.float32)
    own_pieces = tri_panels.reshape(blocks, size, size)
    own_diag = lax.dynamic_index_in_dim(own_pieces, col_position // row_count, 0, keepdims=False)
    own_diag = jnp.where(col_position % row_count == row_position, own_diag, identity_block)
    own_inverse = jax.scipy.linalg.solve_triangular(own_diag, identity_block, lower=True)
    top = lax.all_gather(tri_panels[: slots * size], "col", axis=1, tiled=True)
    inverses = lax.all_gather(own_inverse, "col", axis=1, tiled=True)
    solved, state_top = run_steps(top, inverses, state_rhs[:slots])
    width = state_rhs.shape[2]
    state_top = state_top.reshape(slots * size, width)
    if slots == blocks:
        return state_top
    below = lax.all_gather(tri_panels[slots * size :], "col", axis=1, tiled=True)
    product = dot(below, solved.reshape(col_count * size, width))
    state_below = state_rhs[slots:].reshape((blocks - slots) * size, width) - product
    return jnp.concatenate([state_top, state_below], 0)


def solution(mesh):
    return jax.shard_map(
        on_device,
        mesh=mesh,
        in_specs=(P("row", "col"), P(("row", "col"), None)),
        out_specs=P("row", "col"),
        check_vma=False,
    )
```

time: 601 us -> 359 us (0.60)
  waiting for transfers between devices: 400 us -> 117 us
  Pallas kernels: 0 us -> 112 us
  local copies, waits for them, and re-layouts: 64.1 us -> 21 us
  matrix products: 64.1 us -> 23.6 us
  blocking collectives: 0 us -> 26.3 us
    psum x8 -> x0, waiting for transfers between devices: 258 us -> none  [broadcast(): return lax.psum(block, axis)]
    pallas_call x0 -> x1, Pallas kernels: none -> 112 us  [run_steps(): pl.pallas_call(functools.partial(steps_kernel, row_count, col_count), out...]
    dot_general x16 -> x1, matrix products: 61.1 us -> 20.6 us  [dot(): return jnp.dot(a, b, precision=HIGHEST, preferred_element_type=jnp.float32)]
    dynamic_slice x16 -> x0, local copies, waits for them, and re-layouts: 27.5 us -> none  [the longest x8 27.3 us: upfront_step(): lax.dynamic_slice_in_dim(own_rows, step_index * block_size, block_size, 1)]
    all_to_all x0 -> x1, blocking collectives: none -> 26.3 us  [on_device(): lax.all_to_all(parted, 'col', split_axis=2, concat_axis=1, tiled=True)]
    all_to_all x1 -> x0, waiting for transfers between devices: 20.6 us -> none  [on_device(): lax.all_to_all(parted, 'col', split_axis=2, concat_axis=1, tiled=True)]
    slice x5 -> x4, local copies, waits for them, and re-layouts: 21.3 us -> 4.89 us  [the longest x1 4.61 us: on_device(): below = lax.all_gather(tri_panels[slots * size:], 'col', axis=1, tiled=True)]
    all_gather x2 -> x3, waiting for transfers between devices: 120 us -> 116 us  [the longest x1 91.7 us: on_device(): top = lax.all_gather(tri_panels[:slots * size], 'col', axis=1, tiled=True)]
  transfers between devices with their start and end apart: 11 -> 3, of which waited for: 11 -> 2; matrix products, arithmetic and copies ran while one was open for 18% -> 4% of each run, Pallas kernels for 0% -> 31%
where the time goes in v1:
time: 359 us
  waiting for transfers between devices  117 us (33%)
  Pallas kernels  112 us (31%)
  other arithmetic  45.1 us (13%)
  blocking collectives  26.3 us (7%)
  matrix products  23.6 us (7%)
  local copies, waits for them, and re-layouts  21 us (6%)
  between operations  13.4 us (4%)
    pallas_call x1, Pallas kernels, run_steps(): pl.pallas_call(functools.partial(steps_kernel, row_count, col_count), out...  112 us
    all_gather x1, waiting for transfers between devices, on_device(): top = lax.all_gather(tri_panels[:slots * size], 'col', axis=1, tiled=True)  91.7 us
    another operation x4, other arithmetic, on_device(): jax.scipy.linalg.solve_triangular(own_diag, identity_block, lower=True)  41.7 us
    all_to_all x1, blocking collectives, on_device(): lax.all_to_all(parted, 'col', split_axis=2, concat_axis=1, tiled=True)  26.3 us
    all_gather x1, waiting for transfers between devices, on_device(): inverses = lax.all_gather(own_inverse, 'col', axis=1, tiled=True)  24.6 us
    dot_general x1, matrix products, dot(): return jnp.dot(a, b, precision=HIGHEST, preferred_element_type=jnp.float32)  20.6 us
    another operation x12, local copies, waits for them, and re-layouts  7.62 us
  transfers between devices with their start and end apart: 3, of which 2 were waited for; matrix products, arithmetic and copies ran while one was open for 4% of the time, Pallas kernels for 31%

profile of v1, /device:TPU:16, one launch (start us, length us, event | category | flops | bytes accessed | tf_op | source)
XLA Modules:
  0.0 358.6 jit_solution(3565549012003538368)
XLA Ops:
  6.8 1.4 fusion.1
  8.2 7.7 %while.1 = (s32[]{:T(128)}, f32[512,512]{1,0:T(8,128)S(1)}, s32[4,2]{0,1:T(2,128)S(1)}, f32[4,128,128]{2,1,0:T(8,128)S(1)}, s32[]{:T(128)}) while((s32[]{:T(128)}, f32[512,512]{1,0:T(8,128)S(1)}, s32[4,2]{0,1:T(2,128)S(1)}, f32[4,128,128]{2,1,0:T(8,128)S(1)}, s32[]{:T(128)}) %tuple.21), condition=%wide.while_cond, body=%wide.while_body.sunk | while | flops 2 | bytes 131189 | solution.py:168
  8.8 1.3 bitcast_dynamic-update-slice_fusion.2
  10.7 1.3 bitcast_dynamic-update-slice_fusion.2
  12.1 0.5 fusion.31
  12.7 1.3 bitcast_dynamic-update-slice_fusion.2
  14.6 1.3 bitcast_dynamic-update-slice_fusion.2
  15.9 39.3 %custom-call.4 = f32[4,128,128]{1,2,0:T(8,128)S(1)} custom-call(f32[4,128,128]{2,1,0:T(8,128)S(1)} %get-tuple-element.16), custom_call_target="InvertDiagBlocksLowerTriangular" | custom-call | tf_op jit(solution)/shard_map/jit(_solve_triangular)/triangular_solve | solution.py:168
  57.2 0.6 convolution_subtract_fusion.2
  58.3 1.0 pad_maximum_fusion
  59.4 4.6 %fusion.22 = (f32[1024,512]{1,0:T(8,128)}, f32[1024,512]{1,0:T(8,128)}) fusion(f32[2048,512]{1,0:T(8,128)} %param.2), kind=kLoop, calls=%fused_computation.38 | loop fusion | bytes 8388608 | tf_op jit(solution)/shard_map/slice | solution.py:176
  64.1 0.7 all-gather.8.cloned.1.call-update
  65.2 0.9 copy.18
  66.1 2.0 reshape.54
  68.1 26.3 %all_to_all.15 = f32[8,1,32768]{2,1,0:T(1,128)S(1)} all-to-all(f32[8,1,32768]{2,1,0:T(1,128)S(1)} %reshape.54), channel_id=1, replica_groups=mesh['row'=4,'col'=8] {'col'}, dimensions={0} | all-to-all | bytes 2097152 | tf_op jit(solution)/shard_map/all_to_all | solution.py:163
  94.9 3.1 reduce
  98.1 1.4 reshape.55
  99.5 0.7 copy.25
  100.4 1.0 copy.22
  101.5 24.6 %all-gather.6.cloned.1.call-done.inverses_ref = f32[512,4096]{1,0:T(8,128)} async-done(((f32[512,512]{1,0:T(8,128)}), f32[512,4096]{1,0:T(8,128)}) %all-gather.6.cloned.1.call-update) | async-done | bytes 8388624 | tf_op jit(solution)/shard_map/all_gather | solution.py:170
  126.1 91.7 %all-gather.4.cloned.1.call-done.panels_ref = f32[1024,4096]{1,0:T(8,128)} async-done(((f32[1024,512]{1,0:T(8,128)}), f32[1024,4096]{1,0:T(8,128)}) %all-gather.4.cloned.1.call-update) | async-done | bytes 16777232 | tf_op jit(solution)/shard_map/all_gather | solution.py:169
  217.7 112.2 %shard_map.28 = (f32[8,512,128]{2,1,0:T(8,128)S(1)}, f32[2,512,128]{2,1,0:T(8,128)S(1)}) custom-call(f32[1024,4096]{1,0:T(8,128)} %all-gather.4.cloned.1.call-done.panels_ref, f32[512,4096]{1,0:T(8,128)} %all-gather.6.cloned.1.call-done.inverses_ref, f32[2,512,128]{2,1,0:T(8,128)S(1)} %bitcast.47), custom_call_target="tpu_custom_call" | custom-call | flops 24159191040 | bytes 25165824 | tf_op jit(solution)/shard_map/pallas_call | solution.py:127
  330.2 20.6 %fusion = f32[1024,128]{0,1:T(8,128)S(1)} fusion(f32[1024,128]{0,1:T(8,128)} %copy.22, f32[4096,128]{1,0:T(8,128)S(1)} %bitcast.46, f32[1024,4096]{1,0:T(8,128)} %all-gather.8.cloned.1.call-done), kind=kOutput, calls=%fused_computation.3 | convolution fusion | flops 6442582016 | bytes 19922944 | tf_op jit(solution)/shard_map/dot_general | solution.py:14
  350.8 1.3 copy.24
  (32 shorter events, 6.2 us)
Async XLA Ops:
  6.5 119.5 %all-gather.6.cloned.1.call-start = ((), (), s32[]{:S(2)}) async-start(), calls=%async_computation.2 | async-start | bytes 9437184 | tf_op jit(solution)/shard_map/all_gather | solution.py:170
  59.3 158.4 %all-gather.4.cloned.1.call-start = ((), (), s32[]{:S(2)}) async-start(), calls=%async_computation.1 | async-start | bytes 18874368 | tf_op jit(solution)/shard_map/all_gather | solution.py:169
  64.0 1.2 copy-start
  64.0 266.1 %all-gather.8.cloned.1.call-start = ((), (), s32[]{:S(2)}) async-start(), calls=%async_computation.3 | async-start | bytes 18874368 | tf_op jit(solution)/shard_map/all_gather | solution.py:176
Sparse Core Ops, SparseCore 0:
  59.5 66.5 all-gather.5
  128.0 89.7 all-gather.3
  219.6 89.7 all-gather.7

commit v2 on v1

--- a/solution.py
+++ b/solution.py
@@ -145,7 +145,7 @@
             collective_id=0, has_side_effects=True, vmem_limit_bytes=48 * 1024 * 1024
         ),
         cost_estimate=pl.CostEstimate(
-            flops=60 * size * size * width * 2 * 6, bytes_accessed=24 << 20, transcendentals=0
+            flops=240 * size * size * width * 2 * 6, bytes_accessed=24 << 20, transcendentals=0
         ),
     )(panels, inverses, state)
 
@@ -167,7 +167,9 @@
     own_diag = jnp.where(col_position % row_count == row_position, own_diag, identity_block)
     own_inverse = jax.scipy.linalg.solve_triangular(own_diag, identity_block, lower=True)
     top = lax.all_gather(tri_panels[: slots * size], "col", axis=1, tiled=True)
+    top, own_inverse = lax.optimization_barrier((top, own_inverse))
     inverses = lax.all_gather(own_inverse, "col", axis=1, tiled=True)
+    inverses, tri_panels = lax.optimization_barrier((inverses, tri_panels))
     solved, state_top = run_steps(top, inverses, state_rhs[:slots])
     width = state_rhs.shape[2]
     state_top = state_top.reshape(slots * size, width)

time: 359 us -> 328 us (0.914)
  waiting for transfers between devices: 117 us -> 94.1 us
  matrix products: 23.6 us -> 19.3 us
    all_gather x1, waiting for transfers between devices: 91.7 us -> 37.9 us  [on_device(): top = lax.all_gather(tri_panels[:slots * size], 'col', axis=1, tiled=True)]
    all_gather x1, waiting for transfers between devices: 24.6 us -> 56.1 us  [on_device(): inverses = lax.all_gather(own_inverse, 'col', axis=1, tiled=True)]
    dot_general x1, matrix products: 20.6 us -> 16.3 us  [dot(): return jnp.dot(a, b, precision=HIGHEST, preferred_element_type=jnp.float32)]
  transfers between devices with their start and end apart: 3 -> 3, of which waited for: 2 -> 2; matrix products, arithmetic and copies ran while one was open for 4% -> 19% of each run, Pallas kernels for 31% -> 33%
where the time goes in v2:
time: 328 us
  Pallas kernels  109 us (33%)
  waiting for transfers between devices  94.1 us (29%)
  other arithmetic  46.1 us (14%)
  blocking collectives  26.4 us (8%)
  local copies, waits for them, and re-layouts  19.9 us (6%)
  matrix products  19.3 us (6%)
  between operations  13.4 us (4%)
    pallas_call x1, Pallas kernels, run_steps(): pl.pallas_call(functools.partial(steps_kernel, row_count, col_count), out...  109 us
    all_gather x1, waiting for transfers between devices, on_device(): inverses = lax.all_gather(own_inverse, 'col', axis=1, tiled=True)  56.1 us
    another operation x4, other arithmetic, on_device(): jax.scipy.linalg.solve_triangular(own_diag, identity_block, lower=True)  41.7 us
    all_gather x1, waiting for transfers between devices, on_device(): top = lax.all_gather(tri_panels[:slots * size], 'col', axis=1, tiled=True)  37.9 us
    all_to_all x1, blocking collectives, on_device(): lax.all_to_all(parted, 'col', split_axis=2, concat_axis=1, tiled=True)  26.4 us
    dot_general x1, matrix products, dot(): return jnp.dot(a, b, precision=HIGHEST, preferred_element_type=jnp.float32)  16.3 us
    another operation x12, local copies, waits for them, and re-layouts  7.94 us
  transfers between devices with their start and end apart: 3, of which 2 were waited for; matrix products, arithmetic and copies ran while one was open for 19% of the time, Pallas kernels for 33%

profile of v2, /device:TPU:16, one launch (start us, length us, event | category | flops | bytes accessed | tf_op | source)
XLA Modules:
  0.0 328.1 jit_solution(2329277960577309489)
XLA Ops:
  6.5 3.1 slice.49
  9.8 1.4 fusion
  11.1 8.0 %while.1 = (s32[]{:T(128)}, f32[512,512]{1,0:T(8,128)S(1)}, s32[4,2]{0,1:T(2,128)S(1)}, f32[4,128,128]{2,1,0:T(8,128)S(1)}, s32[]{:T(128)}) while((s32[]{:T(128)}, f32[512,512]{1,0:T(8,128)S(1)}, s32[4,2]{0,1:T(2,128)S(1)}, f32[4,128,128]{2,1,0:T(8,128)S(1)}, s32[]{:T(128)}) %tuple.24), condition=%wide.while_cond, body=%wide.while_body.sunk | while | flops 2 | bytes 131189 | solution.py:168
  11.2 0.6 fusion.29
  11.8 1.3 bitcast_dynamic-update-slice_fusion.2
  13.2 0.6 fusion.29
  13.8 1.3 bitcast_dynamic-update-slice_fusion.2
  15.8 1.3 bitcast_dynamic-update-slice_fusion.2
  17.8 1.3 bitcast_dynamic-update-slice_fusion.2
  19.2 39.3 %custom-call.4 = f32[4,128,128]{1,2,0:T(8,128)S(1)} custom-call(f32[4,128,128]{2,1,0:T(8,128)S(1)} %get-tuple-element.24), custom_call_target="InvertDiagBlocksLowerTriangular" | custom-call | tf_op jit(solution)/shard_map/jit(_solve_triangular)/triangular_solve | solution.py:168
  60.7 0.6 convolution_subtract_fusion.3
  61.8 1.0 pad_maximum_fusion
  62.8 37.9 %all-gather.4.cloned.1.call-done.panels_ref = f32[1024,4096]{1,0:T(8,128)} async-done(((f32[1024,512]{1,0:T(8,128)}), f32[1024,4096]{1,0:T(8,128)}) %all-gather.4.cloned.1.call-update) | async-done | bytes 16777232 | tf_op jit(solution)/shard_map/all_gather | solution.py:169
  100.8 56.1 %all-gather.6.cloned.1.call-done.inverses_ref = f32[512,4096]{1,0:T(8,128)} async-done(((f32[512,512]{1,0:T(8,128)}), f32[512,4096]{1,0:T(8,128)}) %all-gather.6.cloned.1.call-update) | async-done | bytes 8388624 | tf_op jit(solution)/shard_map/all_gather | solution.py:171
  156.9 3.1 slice.53
  160.1 0.9 copy.9
  161.0 2.0 reshape.54
  163.0 26.4 %all_to_all.15 = f32[8,1,32768]{2,1,0:T(1,128)S(1)} all-to-all(f32[8,1,32768]{2,1,0:T(1,128)S(1)} %reshape.54), channel_id=1, replica_groups=mesh['row'=4,'col'=8] {'col'}, dimensions={0} | all-to-all | bytes 2097152 | tf_op jit(solution)/shard_map/all_to_all | solution.py:163
  189.9 3.1 reduce
  193.1 1.4 reshape.55
  194.5 0.7 copy.13
  195.5 108.8 %shard_map.28 = (f32[8,512,128]{2,1,0:T(8,128)S(1)}, f32[2,512,128]{2,1,0:T(8,128)S(1)}) custom-call(f32[1024,4096]{1,0:T(8,128)} %all-gather.4.cloned.1.call-done.panels_ref, f32[512,4096]{1,0:T(8,128)} %all-gather.6.cloned.1.call-done.inverses_ref, f32[2,512,128]{2,1,0:T(8,128)S(1)} %bitcast.43), custom_call_target="tpu_custom_call" | custom-call | flops 96636764160 | bytes 25165824 | tf_op jit(solution)/shard_map/pallas_call | solution.py:127
  304.3 16.3 %convolution_subtract_fusion = f32[1024,128]{1,0:T(8,128)S(1)} fusion(f32[1024,128]{1,0:T(8,128)S(1)} %bitcast.49, f32[1024,4096]{1,0:T(8,128)} %all-gather.8.cloned.1.call-done, f32[4096,128]{1,0:T(8,128)S(1)} %bitcast.42), kind=kOutput, calls=%fused_computation.2 | convolution fusion | flops 6442582016 | bytes 19922944 | tf_op jit(solution)/shard_map/dot_general | solution.py:14
  320.6 1.0 pad_maximum_fusion.1
  (30 shorter events, 5.0 us)
Async XLA Ops:
  6.5 94.2 %all-gather.4.cloned.1.call-start = ((), (), s32[]{:S(2)}) async-start(), calls=%async_computation.1 | async-start | bytes 18874368 | tf_op jit(solution)/shard_map/all_gather | solution.py:169
  9.7 147.3 %all-gather.6.cloned.1.call-start = ((), (), s32[]{:S(2)}) async-start(), calls=%async_computation.2 | async-start | bytes 9437184 | tf_op jit(solution)/shard_map/all_gather | solution.py:171
  62.8 97.3 %copy-start = (f32[256,1024]{1,0:T(8,128)S(1)}, f32[256,1024]{1,0:T(8,128)}, u32[]{:S(2)}) copy-start(f32[256,1024]{1,0:T(8,128)} %param.3) | copy-start | bytes 3145732
  100.8 203.5 %all-gather.8.cloned.1.call-start = ((), (), s32[]{:S(2)}) async-start(), calls=%async_computation.3 | async-start | bytes 18874368 | tf_op jit(solution)/shard_map/all_gather | solution.py:178
Sparse Core Ops, SparseCore 0:
  9.8 90.9 all-gather.3
  102.6 54.2 all-gather.5
  160.2 97.2 all-gather.7
